TPU v7x, 256 devices: a whole 4x4x8 slice. The times are simulated.
256 devices in a mesh: rows: 4 (over x_hi, core), vec: 64 (over y, x_lo, z).
Axes of the slice: x: 4 (x_hi: 2, x_lo: 2; x = x_hi * 2 + x_lo), y: 4, z: 8, core: 2. Of those that a mesh axis runs over, the one named last changes fastest.
Arguments:
- eigen_rows: float32 [2048, 8192], P('rows', 'vec'), may hold values from -6 to 6
- panels: float32 [3, 2048, 256], P(None, ('rows', 'vec')), may hold values from -0.25 to 0.25
Outputs:
- transformed: float32 [2048, 8192], P('rows', 'vec')
All inputs are finite; a program needn't handle non-finite values.
Results may differ from a plain program's by a relative error of at most 0.00017.
Values sent between devices are 32-bit elements; how exact they have to be, the bound alone decides.
No kernel may reach another device: no remote copies, remote signals or barrier semaphores. Data moves between devices by JAX's collectives and lax.ppermute only.
A program may use at most 192 MiB of HBM per device.

v0:
```python
import jax
import jax.numpy as jnp
from jax import lax
from jax.experimental import pallas as pl
from jax.experimental.pallas import tpu as pltpu
from jax.sharding import Mesh, PartitionSpec as P

R = 256
H = 128
Q = 64
F32 = jnp.float32
BF16 = jnp.bfloat16


def halves(value):
    top = value.astype(BF16)
    return top, (value - top.astype(F32)).astype(BF16)


def dot(a, b):
    return jnp.dot(a, b, preferred_element_type=F32)


def product(a, b):
    return dot(a[0], b[0]) + (dot(a[0], b[1]) + dot(a[1], b[0]))


def exact(a, b):
    return jnp.dot(a, b, precision=lax.Precision.HIGHEST, preferred_element_type=F32)


def iota(shape, dim):
    return lax.broadcasted_iota(jnp.int32, shape, dim)


def with_eye(rows):
    return rows + (iota(rows.shape, 0) == iota(rows.shape, 1)).astype(F32)


def spread(tile, column):
    lanes = iota(tile.shape, 1)
    return jnp.take_along_axis(tile, (lanes & ~(Q - 1)) + column, axis=1)


def invert_unit(v00, v01, v11):
    low = iota((Q, H), 1) < Q
    out = []
    for v in (v00, v11):
        packed = jnp.where(low, v[:Q], v[Q:])
        strips = [packed[8 * i : 8 * i + 8] for i in range(Q // 8)]
        result = [
            ((iota((8, H), 1) & (Q - 1)) == iota((8, H), 0) + 8 * i).astype(F32)
            for i in range(Q // 8)
        ]
        for j in range(Q - 1, 0, -1):
            row = result[j // 8][j % 8 : j % 8 + 1]
            for i in range((j - 1) // 8 + 1):
                column = spread(strips[i], j)
                if i == j // 8:
                    column = jnp.where(iota((8, H), 0) < j % 8, column, 0.0)
                result[i] = result[i] - column * row
        packed = jnp.concatenate(result, axis=0)
        top = jnp.where(low, packed, 0.0)
        bottom = jnp.where(low, 0.0, packed)
        corner = jnp.where(low, 0.0, v[:Q])
        part = exact(corner, jnp.concatenate([top, bottom], axis=0))
        part = exact(top, jnp.concatenate([part, jnp.zeros_like(part)], axis=0))
        out.append(jnp.concatenate([top - part, bottom], axis=0))
    t00, t11 = out
    return t00, -exact(t00, exact(v01, t11)), t11


def inverse_of(g00, g01, g11, d00, d11):
    above = iota((H, H), 0) < iota((H, H), 1)
    eye = iota((H, H), 0) == iota((H, H), 1)
    r0, r1 = 2.0 / d00, 2.0 / d11
    v00 = jnp.where(above, g00 * r0, 0.0)
    v11 = jnp.where(above, g11 * r1, 0.0)
    t00, t01, t11 = invert_unit(v00, g01 * r1, v11)
    c0 = jnp.sum(jnp.where(eye, r0, 0.0), axis=1, keepdims=True)
    c1 = jnp.sum(jnp.where(eye, r1, 0.0), axis=1, keepdims=True)
    top = jnp.concatenate([t00 * c0, t01 * c0], axis=1)
    bottom = jnp.concatenate([jnp.zeros((H, H), F32), t11 * c1], axis=1)
    return jnp.concatenate([top, bottom], axis=0)


def diagonal(block):
    eye = iota((H, H), 0) == iota((H, H), 1)
    return jnp.sum(jnp.where(eye, block, 0.0), axis=0, keepdims=True)


def inverse_full(g):
    g00, g01, g11 = g[:H, :H], g[:H, H:], g[H:, H:]
    return inverse_of(g00, g01, g11, diagonal(g00), diagonal(g11))


def pack(g):
    keep = iota((H, H), 0) <= iota((H, H), 1)
    first = jnp.where(keep, g[:H, :H], g[H:, H:])
    diag = jnp.broadcast_to(diagonal(g[H:, H:]), (8, H))
    tail = jnp.concatenate([diag, jnp.zeros((8, H), F32)], axis=1)
    return jnp.concatenate([jnp.concatenate([first, g[:H, H:]], axis=1), tail], axis=0)


def inverse_packed(m, live):
    first, d11 = m[:H, :H], m[H : H + 1, :H]
    d00 = diagonal(first)
    one = jnp.where(live, 0.0, 1.0)
    return inverse_of(first, m[:H, H:], first.T, d00 + one, d11 + one)


def panel(ref, s):
    return ref[:, :, s].reshape(2 * R, R)


def gram_kernel(y_ref, low_ref, up_ref):
    rows = panel(y_ref, 1)
    for half, ref in ((with_eye(rows[R:]), low_ref), (rows[:R], up_ref)):
        ref[...] = pack(product(halves(half.T), halves(half)))


def first_kernel(y_ref, z_ref, out_ref, low_ref, up_ref):
    y = with_eye(panel(y_ref, 0))
    yh, yt = halves(y), halves(y.T)
    z = z_ref[...]
    p = product(yt, halves(z))
    t = inverse_full(product(yt, yh))
    x = product(halves(t), halves(p))
    z = z - product(yh, halves(x))
    out_ref[...] = z
    rows = panel(y_ref, 1)
    low_ref[...] = product(halves(with_eye(rows[R:]).T), halves(z[R:]))
    up_ref[...] = product(halves(rows[:R].T), halves(z[:R]))


def inverse_kernel(live_ref, low_ref, low_in_ref, up_ref, up_in_ref, y_ref, t_low_ref, t_up_ref, t_ref):
    t_low_ref[...] = inverse_packed(low_ref[...] + low_in_ref[...], live_ref[0] != 0)
    t_up_ref[...] = inverse_packed(up_ref[...] + up_in_ref[...], live_ref[1] != 0)
    y = with_eye(panel(y_ref, 2))
    t_ref[...] = inverse_full(product(halves(y.T), halves(y)))


def last_kernel(live_ref, y_ref, z_ref, low_ref, low_in_ref, up_ref, up_in_ref, t_low_ref, t_up_ref, t_ref, out_ref):
    rows = panel(y_ref, 1)
    z = z_ref[...]
    x_low = product(halves(t_low_ref[...]), halves(low_ref[...] + low_in_ref[...]))
    x_up = product(halves(t_up_ref[...]), halves(up_ref[...] + up_in_ref[...]))
    z_low = z[R:] - product(halves(with_eye(rows[R:])), halves(x_low))
    z_up = z[:R] - product(halves(rows[:R]), halves(x_up))
    z_low = jnp.where(live_ref[0] != 0, z_low, z[R:])
    z_up = jnp.where(live_ref[1] != 0, z_up, z[:R])
    z = jnp.concatenate([z_up, z_low], axis=0)
    y = with_eye(panel(y_ref, 2))
    p = product(halves(y.T), halves(z))
    x = product(halves(t_ref[...]), halves(p))
    out_ref[...] = z - product(halves(y), halves(x))


VM = pl.BlockSpec(memory_space=pltpu.VMEM)
SM = pl.BlockSpec(memory_space=pltpu.SMEM)


def call(kernel, outs, args, flops, scalars=0):
    return pl.pallas_call(
        kernel,
        out_shape=[jax.ShapeDtypeStruct(s, F32) for s in outs],
        in_specs=[SM] * scalars + [VM] * (len(args) - scalars),
        out_specs=[VM] * len(outs),
        cost_estimate=pl.CostEstimate(flops=flops, bytes_accessed=4 << 20, transcendentals=0),
        name=kernel.__name__,
    )(*args)


def copies(value, axes):
    count = lax.axis_size(axes)
    stack = jnp.broadcast_to(value, (count, *value.shape))
    return lax.all_to_all(stack, axes, split_axis=0, concat_axis=0, tiled=True)


def rows_shift(value, step):
    route = [(i, i + step) for i in range(4) if 0 <= i + step < 4]
    return lax.ppermute(value, ("xh", "core"), route)


def local(eigen_rows, panels):
    group = lax.axis_index("xh") * 2 + lax.axis_index("core")
    live = jnp.stack([group < 3, group > 0]).astype(jnp.int32)
    near = copies(panels, "z")
    y = copies(near, ("y", "xl"))
    y = y.reshape(8, 8, 3, 8, R)
    columns = eigen_rows.shape[1]
    big = 10**9
    low, up = call(gram_kernel, [(H + 8, R)] * 2, [y], big)
    low_in, up_in = rows_shift(up, -1), rows_shift(low, 1)
    z, p_low, p_up = call(
        first_kernel, [eigen_rows.shape, (R, columns), (R, columns)], [y, eigen_rows], 4 * big
    )
    p_low_in, p_up_in = rows_shift(p_up, -1), rows_shift(p_low, 1)
    ts = call(inverse_kernel, [(R, R)] * 3, [live, low, low_in, up, up_in, y], 4 * big, 1)
    (out,) = call(
        last_kernel,
        [eigen_rows.shape],
        [live, y, z, p_low, p_low_in, p_up, p_up_in, *ts],
        2 * big,
        1,
    )
    return out


def solution(mesh):
    fine = Mesh(mesh.devices.reshape(2, 2, 4, 2, 8), ("xh", "core", "y", "xl", "z"))
    slab = P(("xh", "core"), ("y", "xl", "z"))
    strips = P(None, ("xh", "core", "y", "xl", "z"), None)
    return jax.shard_map(local, mesh=fine, in_specs=(slab, strips), out_specs=slab, check_vma=False)
```

profile of v0, /device:TPU:1, one launch (start us, length us, event | category | flops | bytes accessed | tf_op | source)
XLA Modules:
  0.0 86.2 jit_solution(16786168510254215352)
XLA Ops:
  0.0 0.8 broadcast_in_dim.6
  0.8 17.8 %all_to_all.10 = f32[8,3,8,256]{3,2,1,0:T(8,128)S(1)} all-to-all(f32[8,3,8,256]{3,2,1,0:T(8,128)S(1)} %broadcast_in_dim.6), channel_id=1, replica_groups=mesh['xh'=2,'core'=2,'y'=4,'xl'=2,'z'=8] {'z'}, dimensions={0} | all-to-all | bytes 393216 | tf_op jit(solution)/shard_map/all_to_all | solution.py:177
  18.5 1.3 %broadcast_in_dim.7 = f32[8,8,3,8,256]{4,3,2,1,0:T(8,128)} broadcast(f32[8,3,8,256]{3,2,1,0:T(8,128)S(1)} %all_to_all.10), dimensions={1,2,3,4} | broadcast | bytes 1769472 | tf_op jit(solution)/shard_map/broadcast_in_dim | solution.py:176
  19.8 5.1 %all-to-all-start.1 = ((f32[8,8,3,8,256]{4,3,2,1,0:T(8,128)}), f32[8,8,3,8,256]{4,3,2,1,0:T(8,128)S(1)}, u32[]{:S(2)}, u32[]{:S(2)}) async-start(f32[8,8,3,8,256]{4,3,2,1,0:T(8,128)} %broadcast_in_dim.7), calls=%async_computation.1 | async-start | bytes 3145728 | tf_op jit(solution)/shard_map/all_to_all | solution.py:177
  25.0 0.6 add_convert_fusion.live_ref
  25.5 18.2 %all-to-all-done.1.y_ref = f32[8,8,3,8,256]{4,3,2,1,0:T(8,128)S(1)} async-done(((f32[8,8,3,8,256]{4,3,2,1,0:T(8,128)}), f32[8,8,3,8,256]{4,3,2,1,0:T(8,128)S(1)}, u32[]{:S(2)}, u32[]{:S(2)}) %all-to-all-start.1) | async-done | bytes 1572896 | tf_op jit(solution)/shard_map/all_to_all | solution.py:177
  43.8 0.0 copy-start
  43.8 1.2 %copy-done = f32[8,8,3,8,256]{4,3,2,1,0:T(8,128)} copy-done((f32[8,8,3,8,256]{4,3,2,1,0:T(8,128)}, f32[8,8,3,8,256]{4,3,2,1,0:T(8,128)S(1)}, u32[]{:S(2)}) %copy-start) | copy-done | bytes 1572888
  44.9 2.6 %gram_kernel.1 = (f32[136,256]{1,0:T(8,128)}, f32[136,256]{1,0:T(8,128)}) custom-call(f32[8,8,3,8,256]{4,3,2,1,0:T(8,128)} %copy-done), custom_call_target="tpu_custom_call" | custom-call | flops 1000000000 | bytes 4194304 | tf_op jit(solution)/shard_map/gram_kernel/pallas_call | solution.py:164
  47.5 7.8 %collective-permute-start.3 = (f32[136,256]{1,0:T(8,128)}, f32[136,256]{1,0:T(8,128)S(1)}, u32[]{:S(2)}, u32[]{:S(2)}) collective-permute-start(f32[136,256]{1,0:T(8,128)} %get-tuple-element.16.low_ref), channel_id=1, source_target_pairs={{0,64},{64,128},{128,192},{1,65},{65,129},{129,193},{2,66},{66,130... | collective-permute-start | bytes 417800 | tf_op jit(solution)/shard_map/ppermute | solution.py:182
  55.3 1.9 %collective-permute-start.2 = (f32[136,256]{1,0:T(8,128)}, f32[136,256]{1,0:T(8,128)S(1)}, u32[]{:S(2)}, u32[]{:S(2)}) collective-permute-start(f32[136,256]{1,0:T(8,128)} %get-tuple-element.17.up_ref), channel_id=1, source_target_pairs={{64,0},{128,64},{192,128},{65,1},{129,65},{193,129},{66,2},{130,66... | collective-permute-start | bytes 417800 | tf_op jit(solution)/shard_map/ppermute | solution.py:182
  57.2 6.7 %first_kernel.1 = (f32[512,128]{1,0:T(8,128)}, f32[256,128]{1,0:T(8,128)}, f32[256,128]{1,0:T(8,128)}) custom-call(f32[8,8,3,8,256]{4,3,2,1,0:T(8,128)} %copy-done, f32[512,128]{1,0:T(8,128)} %z_ref.1), custom_call_target="tpu_custom_call" | custom-call | flops 4000000000 | bytes 4194304 | tf_op jit(solution)/shard_map/first_kernel/pallas_call | solution.py:164
  63.9 5.1 %collective-permute-start.1 = (f32[256,128]{1,0:T(8,128)}, f32[256,128]{1,0:T(8,128)S(1)}, u32[]{:S(2)}, u32[]{:S(2)}) collective-permute-start(f32[256,128]{1,0:T(8,128)} %get-tuple-element.14.low_ref), channel_id=1, source_target_pairs={{0,64},{64,128},{128,192},{1,65},{65,129},{129,193},{2,66},{66,130... | collective-permute-start | bytes 393224 | tf_op jit(solution)/shard_map/ppermute | solution.py:182
  69.0 1.9 %collective-permute-start = (f32[256,128]{1,0:T(8,128)}, f32[256,128]{1,0:T(8,128)S(1)}, u32[]{:S(2)}, u32[]{:S(2)}) collective-permute-start(f32[256,128]{1,0:T(8,128)} %get-tuple-element.15.up_ref), channel_id=1, source_target_pairs={{64,0},{128,64},{192,128},{65,1},{129,65},{193,129},{66,2},{130,66... | collective-permute-start | bytes 393224 | tf_op jit(solution)/shard_map/ppermute | solution.py:182
  70.9 0.0 collective-permute-done.3.up_in_ref
  71.0 0.0 copy-start.1
  71.0 0.0 collective-permute-done.2.low_in_ref
  71.0 0.6 copy-done.1
  71.6 0.0 copy-start.2
  71.6 0.7 copy-done.2
  72.3 9.0 %inverse_kernel.1 = (f32[256,256]{1,0:T(8,128)}, f32[256,256]{1,0:T(8,128)}, f32[256,256]{1,0:T(8,128)}) custom-call(s32[2]{0:T(128)} %add_convert_fusion.live_ref, f32[136,256]{1,0:T(8,128)} %get-tuple-element.16.low_ref, f32[136,256]{1,0:T(8,128)} %copy-done.2, f32[136,256]{1,0:T(8,128)} %get-tuple-element.17.up_ref, f32[136,256]{1,0:T(8,128)} %copy-done.1, ...), custom_call_target="tpu_custom_call" | custom-call | flops 4000000000 | bytes 4194304 | tf_op jit(solution)/shard_map/inverse_kernel/pallas_call | solution.py:164
  81.3 0.0 collective-permute-done.1.up_in_ref
  81.3 0.0 copy-start.3
  81.3 0.0 collective-permute-done.low_in_ref
  81.3 0.0 copy-start.4
  81.3 0.6 copy-done.3
  81.9 0.1 copy-done.4
  82.0 4.2 %last_kernel.1 = f32[512,128]{1,0:T(8,128)} custom-call(s32[2]{0:T(128)} %add_convert_fusion.live_ref, f32[8,8,3,8,256]{4,3,2,1,0:T(8,128)} %copy-done, f32[512,128]{1,0:T(8,128)} %get-tuple-element.13.z_ref, f32[256,128]{1,0:T(8,128)} %get-tuple-element.14.low_ref, f32[256,128]{1,0:T(8,128)} %copy-done.4, f32[256,128]{1,0:T(8,128)} %get-tuple-element.15.up_ref, ...), custom_call_target="tpu_custom_call" | custom-call | flops 2000000000 | bytes 4194304 | tf_op jit(solution)/shard_map/last_kernel/pallas_call | solution.py:164
Async XLA Ops:
  19.8 23.9 %all-to-all-start.1 = ((f32[8,8,3,8,256]{4,3,2,1,0:T(8,128)}), f32[8,8,3,8,256]{4,3,2,1,0:T(8,128)S(1)}, u32[]{:S(2)}, u32[]{:S(2)}) async-start(f32[8,8,3,8,256]{4,3,2,1,0:T(8,128)} %broadcast_in_dim.7), calls=%async_computation.1 | async-start | bytes 3145728 | tf_op jit(solution)/shard_map/all_to_all | solution.py:177
  43.8 1.2 %copy-start = (f32[8,8,3,8,256]{4,3,2,1,0:T(8,128)}, f32[8,8,3,8,256]{4,3,2,1,0:T(8,128)S(1)}, u32[]{:S(2)}) copy-start(f32[8,8,3,8,256]{4,3,2,1,0:T(8,128)S(1)} %all-to-all-done.1.y_ref) | copy-start | bytes 4718596
  47.5 23.4 %collective-permute-start.3 = (f32[136,256]{1,0:T(8,128)}, f32[136,256]{1,0:T(8,128)S(1)}, u32[]{:S(2)}, u32[]{:S(2)}) collective-permute-start(f32[136,256]{1,0:T(8,128)} %get-tuple-element.16.low_ref), channel_id=1, source_target_pairs={{0,64},{64,128},{128,192},{1,65},{65,129},{129,193},{2,66},{66,130... | collective-permute-start | bytes 417800 | tf_op jit(solution)/shard_map/ppermute | solution.py:182
  55.3 15.7 %collective-permute-start.2 = (f32[136,256]{1,0:T(8,128)}, f32[136,256]{1,0:T(8,128)S(1)}, u32[]{:S(2)}, u32[]{:S(2)}) collective-permute-start(f32[136,256]{1,0:T(8,128)} %get-tuple-element.17.up_ref), channel_id=1, source_target_pairs={{64,0},{128,64},{192,128},{65,1},{129,65},{193,129},{66,2},{130,66... | collective-permute-start | bytes 417800 | tf_op jit(solution)/shard_map/ppermute | solution.py:182
  63.9 17.4 %collective-permute-start.1 = (f32[256,128]{1,0:T(8,128)}, f32[256,128]{1,0:T(8,128)S(1)}, u32[]{:S(2)}, u32[]{:S(2)}) collective-permute-start(f32[256,128]{1,0:T(8,128)} %get-tuple-element.14.low_ref), channel_id=1, source_target_pairs={{0,64},{64,128},{128,192},{1,65},{65,129},{129,193},{2,66},{66,130... | collective-permute-start | bytes 393224 | tf_op jit(solution)/shard_map/ppermute | solution.py:182
  69.0 12.3 %collective-permute-start = (f32[256,128]{1,0:T(8,128)}, f32[256,128]{1,0:T(8,128)S(1)}, u32[]{:S(2)}, u32[]{:S(2)}) collective-permute-start(f32[256,128]{1,0:T(8,128)} %get-tuple-element.15.up_ref), channel_id=1, source_target_pairs={{64,0},{128,64},{192,128},{65,1},{129,65},{193,129},{66,2},{130,66... | collective-permute-start | bytes 393224 | tf_op jit(solution)/shard_map/ppermute | solution.py:182
  71.0 0.7 copy-start.1
  71.6 0.7 copy-start.2
  81.3 0.7 copy-start.3
  81.3 0.7 copy-start.4
where the time goes:
time: 86.7 us; the launch traced here: 86.2 us
  Pallas kernels  22.5 us (26%)
  starting transfers between devices  21.8 us (25%)
  waiting for transfers between devices  18.2 us (21%)
  blocking collectives  17.8 us (21%)
  local copies, waits for them, and re-layouts  5.21 us (6%)
    pallas_call x4, Pallas kernels, call(): pl.pallas_call(kernel, out_shape=[jax.ShapeDtypeStruct(s, F32) for s in o...  22.5 us
    all_to_all x1, waiting for transfers between devices, copies(): return lax.all_to_all(stack, axes, split_axis=0, concat_axis=0, tiled=True)  18.2 us
    all_to_all x1, blocking collectives, copies(): return lax.all_to_all(stack, axes, split_axis=0, concat_axis=0, tiled=True)  17.8 us
    ppermute x4, starting transfers between devices, rows_shift(): return lax.ppermute(value, ('xh', 'core'), route)  16.7 us
    all_to_all x1, starting transfers between devices, copies(): return lax.all_to_all(stack, axes, split_axis=0, concat_axis=0, tiled=True)  5.12 us
    unnamed x10, local copies, waits for them, and re-layouts  3.16 us
    broadcast_in_dim x2, local copies, waits for them, and re-layouts, copies(): stack = jnp.broadcast_to(value, (count, *value.shape))  2.05 us
  transfers between devices with their start and end apart: 5, of which 1 were waited for; matrix products, arithmetic and copies ran while one was open for 1% of the time, Pallas kernels for 18%

commit v1 on v0

v1 whole, which is shorter than its diff:
```python
import jax
import jax.numpy as jnp
from jax import lax
from jax.experimental import pallas as pl
from jax.experimental.pallas import tpu as pltpu
from jax.sharding import Mesh, PartitionSpec as P

R = 256
H = 128
Q = 32
F32 = jnp.float32
BF16 = jnp.bfloat16


def halves(value):
    top = value.astype(BF16)
    return top, (value - top.astype(F32)).astype(BF16)


def dot(a, b):
    return jnp.dot(a, b, preferred_element_type=F32)


def product(a, b):
    return dot(a[0], b[0]) + (dot(a[0], b[1]) + dot(a[1], b[0]))


def exact(a, b):
    return jnp.dot(a, b, precision=lax.Precision.HIGHEST, preferred_element_type=F32)


def iota(shape, dim):
    return lax.broadcasted_iota(jnp.int32, shape, dim)


def with_eye(rows):
    return rows + (iota(rows.shape, 0) == iota(rows.shape, 1)).astype(F32)


def spread(tile, column):
    lanes = iota(tile.shape, 1)
    return jnp.take_along_axis(tile, (lanes & ~(Q - 1)) + column, axis=1)


def invert_units(blocks):
    lanes, count = iota((8, H), 1), Q // 8
    strips, results = [], []
    for v in blocks:
        for i in range(count):
            strip = v[8 * i : 8 * i + 8]
            for k in range(1, H // Q):
                strip = jnp.where(lanes >= k * Q, v[k * Q + 8 * i : k * Q + 8 * i + 8], strip)
            strips.append(strip)
            results.append(((lanes & (Q - 1)) == iota((8, H), 0) + 8 * i).astype(F32))
    for j in range(Q - 1, 0, -1):
        for m in range(0, len(strips), count):
            row = results[m + j // 8][j % 8 : j % 8 + 1]
            for i in range((j - 1) // 8 + 1):
                column = spread(strips[m + i], j)
                if i == j // 8:
                    column = jnp.where(iota((8, H), 0) < j % 8, column, 0.0)
                results[m + i] = results[m + i] - column * row
    wide = iota((Q, H), 1)
    out = []
    for m in range(0, len(strips), count):
        packed = jnp.concatenate(results[m : m + count], axis=0)
        out.append(
            jnp.concatenate(
                [
                    jnp.where((wide >= k * Q) & (wide < (k + 1) * Q), packed, 0.0)
                    for k in range(H // Q)
                ],
                axis=0,
            )
        )
    span = Q
    rows, cols = iota((H, H), 0), iota((H, H), 1)
    while span < H:
        corner = ((rows & span) == 0) & ((cols & span) != 0)
        corner = corner & ((rows & ~(2 * span - 1)) == (cols & ~(2 * span - 1)))
        parts = [exact(t, jnp.where(corner, v, 0.0)) for t, v in zip(out, blocks)]
        out = [t - exact(part, t) for t, part in zip(out, parts)]
        span *= 2
    return out


def invert_unit_all(matrices):
    out = invert_units([v for v00, _, v11 in matrices for v in (v00, v11)])
    tops, bottoms = out[0::2], out[1::2]
    corners = [exact(v01, t11) for (_, v01, _), t11 in zip(matrices, bottoms)]
    corners = [-exact(t00, c) for t00, c in zip(tops, corners)]
    return list(zip(tops, corners, bottoms))


def inverses_of(grams):
    above = iota((H, H), 0) < iota((H, H), 1)
    eye = iota((H, H), 0) == iota((H, H), 1)
    units, scales = [], []
    for g00, g01, g11, d00, d11 in grams:
        r0, r1 = 2.0 / d00, 2.0 / d11
        units.append(
            (jnp.where(above, g00 * r0, 0.0), g01 * r1, jnp.where(above, g11 * r1, 0.0))
        )
        scales.append(
            [jnp.sum(jnp.where(eye, r, 0.0), axis=1, keepdims=True) for r in (r0, r1)]
        )
    out = []
    for (t00, t01, t11), (c0, c1) in zip(invert_unit_all(units), scales):
        top = jnp.concatenate([t00 * c0, t01 * c0], axis=1)
        bottom = jnp.concatenate([jnp.zeros((H, H), F32), t11 * c1], axis=1)
        out.append(jnp.concatenate([top, bottom], axis=0))
    return out


def diagonal(block):
    eye = iota((H, H), 0) == iota((H, H), 1)
    return jnp.sum(jnp.where(eye, block, 0.0), axis=0, keepdims=True)


def full_parts(g):
    g00, g01, g11 = g[:H, :H], g[:H, H:], g[H:, H:]
    return g00, g01, g11, diagonal(g00), diagonal(g11)


def pack(g):
    keep = iota((H, H), 0) <= iota((H, H), 1)
    first = jnp.where(keep, g[:H, :H], g[H:, H:])
    diag = jnp.broadcast_to(diagonal(g[H:, H:]), (8, H))
    tail = jnp.concatenate([diag, jnp.zeros((8, H), F32)], axis=1)
    return jnp.concatenate([jnp.concatenate([first, g[:H, H:]], axis=1), tail], axis=0)


def packed_parts(m, live):
    first, d11 = m[:H, :H], m[H : H + 1, :H]
    one = jnp.where(live, 0.0, 1.0)
    return first, m[:H, H:], first.T, diagonal(first) + one, d11 + one


def panel(ref, s):
    return ref[:, :, s].reshape(2 * R, R)


def spread_kernel(value_ref, out_ref):
    for i in range(out_ref.shape[0]):
        out_ref[i] = value_ref[...]


def spread_parts_kernel(value_ref, *outs):
    start = 0
    for out_ref in outs:
        stop = start + out_ref.shape[2]
        for i in range(out_ref.shape[0]):
            out_ref[i] = value_ref[:, start:stop]
        start = stop


def gram_kernel(core_ref, g_ref, c_ref, x_ref, yh_ref, yl_ref, th_ref, tl_ref):
    rows = panel(g_ref, 1)
    packed = []
    for k, half in enumerate((rows[:R], with_eye(rows[R:]))):
        y, t = halves(half), halves(half.T)
        packed.append(pack(product(t, y)))
        yh_ref[k], yl_ref[k] = y
        th_ref[k], tl_ref[k] = t
    up, low = packed
    first = core_ref[0] == 0
    c_ref[...] = jnp.where(first, low, up)
    x_ref[...] = jnp.where(first, up, low)


def first_kernel(core_ref, g_ref, z_ref, th_ref, tl_ref, out_ref, c_ref, x_ref):
    y = with_eye(panel(g_ref, 0))
    yh, yt = halves(y), halves(y.T)
    z = z_ref[...]
    p = product(yt, halves(z))
    (t,) = inverses_of([full_parts(product(yt, yh))])
    x = exact(t, p)
    z = z - product(yh, halves(x))
    up = product((th_ref[0], tl_ref[0]), halves(z[:R]))
    low = product((th_ref[1], tl_ref[1]), halves(z[R:]))
    first = core_ref[0] == 0
    c_ref[...] = jnp.where(first, low, up)
    x_ref[...] = jnp.where(first, up, low)
    out_ref[...] = z


def second_kernel(core_ref, g_ref, c_ref, c_in_ref, x_ref, x_in_ref, th_ref, tl_ref, t_ref, tc_ref, tx_ref):
    y = with_eye(panel(g_ref, 0))
    yh, yt = halves(y), halves(y.T)
    th_ref[...], tl_ref[...] = yt
    t_ref[...], tc_ref[...], tx_ref[...] = inverses_of(
        [
            full_parts(product(yt, yh)),
            packed_parts(c_ref[...] + c_in_ref[...], True),
            packed_parts(x_ref[...] + x_in_ref[...], core_ref[1] != 0),
        ]
    )


def last_kernel(core_ref, g_ref, z_ref, c_ref, c_in_ref, x_ref, x_in_ref, tc_ref, tx_ref,
                ah_ref, al_ref, th_ref, tl_ref, t_ref, out_ref):
    xc = exact(tc_ref[...], c_ref[...] + c_in_ref[...])
    xx = exact(tx_ref[...], x_ref[...] + x_in_ref[...])
    xx = jnp.where(core_ref[1] != 0, xx, 0.0)
    first = core_ref[0] == 0
    z_up = z_ref[:R] - product((ah_ref[0], al_ref[0]), halves(jnp.where(first, xx, xc)))
    z_low = z_ref[R:] - product((ah_ref[1], al_ref[1]), halves(jnp.where(first, xc, xx)))
    z = jnp.concatenate([z_up, z_low], axis=0)
    p = product((th_ref[...], tl_ref[...]), halves(z))
    x = exact(t_ref[...], p)
    out_ref[...] = z - product(halves(with_eye(panel(g_ref, 0))), halves(x))


VM = pl.BlockSpec(memory_space=pltpu.VMEM)
SM = pl.BlockSpec(memory_space=pltpu.SMEM)


def call(kernel, outs, args, flops, scalars=0):
    outs = [o if isinstance(o[0], tuple) else (o, F32) for o in outs]
    return pl.pallas_call(
        kernel,
        out_shape=[jax.ShapeDtypeStruct(s, d) for s, d in outs],
        in_specs=[SM] * scalars + [VM] * (len(args) - scalars),
        out_specs=[VM] * len(outs),
        cost_estimate=pl.CostEstimate(flops=flops, bytes_accessed=1 << 20, transcendentals=0),
        compiler_params=pltpu.CompilerParams(vmem_limit_bytes=12 << 20),
        name=kernel.__name__,
    )(*args)


def exchange(stack, axes):
    return lax.all_to_all(stack, axes, split_axis=0, concat_axis=0, tiled=True)


def swap_cores(value):
    return lax.ppermute(value, "core", [(0, 1), (1, 0)])


def swap_middle(value):
    return lax.ppermute(value, ("xh", "core"), [(1, 2), (2, 1)])


def local(eigen_rows, panels):
    core = lax.axis_index("core")
    group = lax.axis_index("xh") * 2 + core
    flags = jnp.stack([core, (group == 1) | (group == 2)]).astype(jnp.int32)
    (stack,) = call(spread_kernel, [(8, *panels.shape)], [panels], 10**6)
    near = exchange(stack, "z")
    early, late = call(
        spread_parts_kernel, [(8, 8, 2, 8, R), (8, 8, 1, 8, R)], [near], 10**6
    )
    every = exchange(early, ("y", "xl"))
    third = exchange(late, ("y", "xl"))
    columns = eigen_rows.shape[1]
    half = ((2, R, R), BF16)
    big = 10**9
    c, x, ah, al, bh, bl = call(
        gram_kernel, [(H + 8, R)] * 2 + [half] * 4, [flags, every], big, 1
    )
    x_in, c_in = swap_middle(x), swap_cores(c)
    z, pc, px = call(
        first_kernel,
        [eigen_rows.shape, (R, columns), (R, columns)],
        [flags, every, eigen_rows, bh, bl],
        8 * big,
        1,
    )
    px_in, pc_in = swap_middle(px), swap_cores(pc)
    th, tl, t, tc, tx = call(
        second_kernel,
        [((R, 2 * R), BF16)] * 2 + [(R, R)] * 3,
        [flags, third, c, c_in, x, x_in],
        8 * big,
        1,
    )
    (out,) = call(
        last_kernel,
        [eigen_rows.shape],
        [flags, third, z, pc, pc_in, px, px_in, tc, tx, ah, al, th, tl, t],
        2 * big,
        1,
    )
    return out


def solution(mesh):
    fine = Mesh(mesh.devices.reshape(2, 2, 4, 2, 8), ("xh", "core", "y", "xl", "z"))
    slab = P(("xh", "core"), ("y", "xl", "z"))
    strips = P(None, ("xh", "core", "y", "xl", "z"), None)
    return jax.shard_map(local, mesh=fine, in_specs=(slab, strips), out_specs=slab, check_vma=False)
```

time: 86.7 us -> 66.8 us (0.77)
  Pallas kernels: 22.5 us -> 14.2 us
  local copies, waits for them, and re-layouts: 5.21 us -> 0.74 us
  waiting for transfers between devices: 18.2 us -> 14.2 us
  starting transfers between devices: 21.8 us -> 19.4 us
    pallas_call x4 -> x6, Pallas kernels: 22.5 us -> 14.2 us  [call(): pl.pallas_call(kernel, out_shape=[jax.ShapeDtypeStruct(s, d) for s, d in...]
    ppermute x4, starting transfers between devices: 16.7 us -> 10.8 us  [the longest x2 7.05 us: swap_middle(): return lax.ppermute(value, ('xh', 'core'), [(1, 2), (2, 1)])]
    all_to_all x1 -> x2, waiting for transfers between devices: 18.2 us -> 13.1 us  [exchange(): return lax.all_to_all(stack, axes, split_axis=0, concat_axis=0, tiled=True)]
    all_to_all x1 -> x2, starting transfers between devices: 5.12 us -> 8.61 us  [exchange(): return lax.all_to_all(stack, axes, split_axis=0, concat_axis=0, tiled=True)]
    unnamed x10 -> x4, local copies, waits for them, and re-layouts: 3.16 us -> 0.74 us
    broadcast_in_dim x2 -> x0, local copies, waits for them, and re-layouts: 2.05 us -> none  [copies(): stack = jnp.broadcast_to(value, (count, *value.shape))]
    ppermute x4, waiting for transfers between devices: 0.01 us -> 1.07 us  [the longest x2 1.07 us: swap_middle(): return lax.ppermute(value, ('xh', 'core'), [(1, 2), (2, 1)])]
  transfers between devices with their start and end apart: 5 -> 6, of which waited for: 1 -> 2; matrix products, arithmetic and copies ran while one was open for 1% -> 0% of each run, Pallas kernels for 18% -> 14%
where the time goes in v1:
time: 66.8 us; the launch traced here: 66.5 us
  starting transfers between devices  19.4 us (29%)
  blocking collectives  17.8 us (27%)
  Pallas kernels  14.2 us (21%)
  waiting for transfers between devices  14.2 us (21%)
  local copies, waits for them, and re-layouts  0.74 us (1%)
    all_to_all x1, blocking collectives, exchange(): return lax.all_to_all(stack, axes, split_axis=0, concat_axis=0, tiled=True)  17.8 us
    pallas_call x6, Pallas kernels, call(): pl.pallas_call(kernel, out_shape=[jax.ShapeDtypeStruct(s, d) for s, d in...  14.2 us
    all_to_all x2, waiting for transfers between devices, exchange(): return lax.all_to_all(stack, axes, split_axis=0, concat_axis=0, tiled=True)  13.1 us
    all_to_all x2, starting transfers between devices, exchange(): return lax.all_to_all(stack, axes, split_axis=0, concat_axis=0, tiled=True)  8.61 us
    ppermute x2, starting transfers between devices, swap_middle(): return lax.ppermute(value, ('xh', 'core'), [(1, 2), (2, 1)])  7.05 us
    ppermute x2, starting transfers between devices, swap_cores(): return lax.ppermute(value, 'core', [(0, 1), (1, 0)])  3.75 us
  transfers between devices with their start and end apart: 6, of which 2 were waited for; matrix products, arithmetic and copies ran while one was open for 0% of the time, Pallas kernels for 14%

profile of v1, /device:TPU:1, one launch (start us, length us, event | category | flops | bytes accessed | tf_op | source)
XLA Modules:
  0.0 66.5 jit_solution(16657870131124527485)
XLA Ops:
  0.0 0.0 copy-start
  0.0 0.7 %copy-done = f32[3,8,256]{2,1,0:T(8,128)S(1)} copy-done((f32[3,8,256]{2,1,0:T(8,128)S(1)}, f32[3,8,256]{2,1,0:T(8,128)}, u32[]{:S(2)}) %copy-start) | copy-done | bytes 24600
  0.8 17.8 %all_to_all.15.value_ref = f32[8,3,8,256]{3,2,1,0:T(8,128)S(1)} all-to-all(f32[8,3,8,256]{3,2,1,0:T(8,128)S(1)} %spread_kernel.1), channel_id=1, replica_groups=mesh['xh'=2,'core'=2,'y'=4,'xl'=2,'z'=8] {'z'}, dimensions={0} | all-to-all | bytes 393216 | tf_op jit(solution)/shard_map/all_to_all | solution.py:232
  18.5 1.2 %spread_parts_kernel.1 = (f32[8,8,2,8,256]{4,3,2,1,0:T(8,128)}, f32[8,8,1,8,256]{4,3,2,1,0:T(8,128)}) custom-call(f32[8,3,8,256]{3,2,1,0:T(8,128)S(1)} %all_to_all.15.value_ref), custom_call_target="tpu_custom_call" | custom-call | flops 1000000 | bytes 1048576 | tf_op jit(solution)/shard_map/spread_parts_kernel/pallas_call | solution.py:220
  19.8 5.1 %all-to-all-start.2 = ((f32[8,8,2,8,256]{4,3,2,1,0:T(8,128)}), f32[8,8,2,8,256]{4,3,2,1,0:T(8,128)S(1)}, u32[]{:S(2)}, u32[]{:S(2)}) async-start(f32[8,8,2,8,256]{4,3,2,1,0:T(8,128)} %get-tuple-element.22), calls=%async_computation.2 | async-start | bytes 2097152 | tf_op jit(solution)/shard_map/all_to_all | solution.py:232
  24.9 0.1 pad_add_fusion.core_ref
  25.0 13.1 %all-to-all-done.2.g_ref = f32[8,8,2,8,256]{4,3,2,1,0:T(8,128)S(1)} async-done(((f32[8,8,2,8,256]{4,3,2,1,0:T(8,128)}), f32[8,8,2,8,256]{4,3,2,1,0:T(8,128)S(1)}, u32[]{:S(2)}, u32[]{:S(2)}) %all-to-all-start.2) | async-done | bytes 1048608 | tf_op jit(solution)/shard_map/all_to_all | solution.py:232
  38.1 3.5 %all-to-all-start.1 = ((f32[8,8,1,8,256]{4,3,2,1,0:T(8,128)}), f32[8,8,1,8,256]{4,3,2,1,0:T(8,128)S(1)}, u32[]{:S(2)}, u32[]{:S(2)}) async-start(f32[8,8,1,8,256]{4,3,2,1,0:T(8,128)} %get-tuple-element.21), calls=%async_computation.1 | async-start | bytes 1048576 | tf_op jit(solution)/shard_map/all_to_all | solution.py:232
  41.6 0.0 copy-start.1
  41.6 1.1 %gram_kernel.1 = (f32[136,256]{1,0:T(8,128)S(1)}, f32[136,256]{1,0:T(8,128)S(1)}, bf16[2,256,256]{2,1,0:T(8,128)(2,1)S(1)}, bf16[2,256,256]{2,1,0:T(8,128)(2,1)S...) custom-call(s32[2]{0:T(128)S(1)} %pad_add_fusion.core_ref, ...), custom_call_target="tpu_custom_call" | custom-call | flops 1000000000 | bytes 1048576 | tf_op jit(solution)/shard_map/gram_kernel/pallas_call | solution.py:220
  42.6 3.7 %collective-permute-start.2 = (f32[136,256]{1,0:T(8,128)S(1)}, f32[136,256]{1,0:T(8,128)S(1)}, u32[]{:S(2)}, u32[]{:S(2)}) collective-permute-start(f32[136,256]{1,0:T(8,128)S(1)} %get-tuple-element.28.c_ref), channel_id=1, source_target_pairs={{0,64},{64,0},{1,65},{65,1},{2,66},{66,2},{3,67},{67,3},{4,68},{68... | collective-permute-start | bytes 417800 | tf_op jit(solution)/shard_map/ppermute | solution.py:236
  46.3 4.3 %collective-permute-start.3 = (f32[136,256]{1,0:T(8,128)S(1)}, f32[136,256]{1,0:T(8,128)S(1)}, u32[]{:S(2)}, u32[]{:S(2)}) collective-permute-start(f32[136,256]{1,0:T(8,128)S(1)} %get-tuple-element.29.x_ref), channel_id=1, source_target_pairs={{64,128},{128,64},{65,129},{129,65},{66,130},{130,66},{67,131},{13... | collective-permute-start | bytes 417800 | tf_op jit(solution)/shard_map/ppermute | solution.py:240
  50.6 0.0 copy-done.1
  50.6 4.4 %first_kernel.1 = (f32[512,128]{1,0:T(8,128)S(1)}, f32[256,128]{1,0:T(8,128)S(1)}, f32[256,128]{1,0:T(8,128)S(1)}) custom-call(s32[2]{0:T(128)S(1)} %pad_add_fusion.core_ref, f32[8,8,2,8,256]{4,3,2,1,0:T(8,128)S(1)} %all-to-all-done.2.g_ref, f32[512,128]{1,0:T(8,128)S(1)} %copy-done.1, bf16[2,256,256]{2,1,0:T(8,128)(2,1)S(1)} %get-tuple-element.23.th_ref, ...), custom_call_target="tpu_custom_call" | custom-call | flops 8000000000 | bytes 1048576 | tf_op jit(solution)/shard_map/first_kernel/pallas_call | solution.py:220
  55.0 0.1 collective-permute-start
  55.1 2.8 %collective-permute-start.1 = (f32[256,128]{1,0:T(8,128)S(1)}, f32[256,128]{1,0:T(8,128)S(1)}, u32[]{:S(2)}, u32[]{:S(2)}) collective-permute-start(f32[256,128]{1,0:T(8,128)S(1)} %get-tuple-element.27.x_ref), channel_id=1, source_target_pairs={{64,128},{128,64},{65,129},{129,65},{66,130},{130,66},{67,131},{13... | collective-permute-start | bytes 393224 | tf_op jit(solution)/shard_map/ppermute | solution.py:240
  57.9 0.0 all-to-all-done.1.g_ref
  57.9 0.0 collective-permute-done.2.c_in_ref
  57.9 0.0 collective-permute-done.3.x_in_ref
  57.9 3.9 %second_kernel.1 = (bf16[256,512]{1,0:T(8,128)(2,1)S(1)}, bf16[256,512]{1,0:T(8,128)(2,1)S(1)}, f32[256,256]{1,0:T(8,128)S(1)}, f32[256,256]{1,0:T(8,128)S(1)}, f32[256,256]{1,0:T(8,128)S(1)}) custom-call(s32[2]{0:T(128)S(1)} %pad_add_fusion.core_ref, f32[8,8,1,8,256]{4,3,2,1,0:T(8,128)S(1)} %all-to-all-done.1.g_ref, ...), custom_call_target="tpu_custom_call" | custom-call | flops 8000000000 | bytes 1048576 | tf_op jit(solution)/shard_map/second_kernel/pallas_call | solution.py:220
  61.8 0.0 collective-permute-done.c_in_ref
  61.8 1.1 %collective-permute-done.1.x_in_ref = f32[256,128]{1,0:T(8,128)S(1)} collective-permute-done((f32[256,128]{1,0:T(8,128)S(1)}, f32[256,128]{1,0:T(8,128)S(1)}, u32[]{:S(2)}, u32[]{:S(2)}) %collective-permute-start.1) | collective-permute-done | bytes 131104 | tf_op jit(solution)/shard_map/ppermute | solution.py:240
  62.9 3.6 %last_kernel.1 = f32[512,128]{1,0:T(8,128)} custom-call(s32[2]{0:T(128)S(1)} %pad_add_fusion.core_ref, f32[8,8,1,8,256]{4,3,2,1,0:T(8,128)S(1)} %all-to-all-done.1.g_ref, f32[512,128]{1,0:T(8,128)S(1)} %get-tuple-element.25.z_ref, f32[256,128]{1,0:T(8,128)S(1)} %get-tuple-element.26.c_ref, f32[256,128]{1,0:T(8,128)S(1)} %collective-permute-done.c_in_ref, ...), custom_call_target="tpu_custom_call" | custom-call | flops 2000000000 | bytes 1048576 | tf_op jit(solution)/shard_map/last_kernel/pallas_call | solution.py:220
  (1 shorter events, 0.0 us)
Async XLA Ops:
  0.0 0.7 %copy-start = (f32[3,8,256]{2,1,0:T(8,128)S(1)}, f32[3,8,256]{2,1,0:T(8,128)}, u32[]{:S(2)}) copy-start(f32[3,8,256]{2,1,0:T(8,128)} %value_ref.1) | copy-start | bytes 73732
  19.8 18.3 %all-to-all-start.2 = ((f32[8,8,2,8,256]{4,3,2,1,0:T(8,128)}), f32[8,8,2,8,256]{4,3,2,1,0:T(8,128)S(1)}, u32[]{:S(2)}, u32[]{:S(2)}) async-start(f32[8,8,2,8,256]{4,3,2,1,0:T(8,128)} %get-tuple-element.22), calls=%async_computation.2 | async-start | bytes 2097152 | tf_op jit(solution)/shard_map/all_to_all | solution.py:232
  38.1 19.8 %all-to-all-start.1 = ((f32[8,8,1,8,256]{4,3,2,1,0:T(8,128)}), f32[8,8,1,8,256]{4,3,2,1,0:T(8,128)S(1)}, u32[]{:S(2)}, u32[]{:S(2)}) async-start(f32[8,8,1,8,256]{4,3,2,1,0:T(8,128)} %get-tuple-element.21), calls=%async_computation.1 | async-start | bytes 1048576 | tf_op jit(solution)/shard_map/all_to_all | solution.py:232
  41.6 9.0 %copy-start.1 = (f32[512,128]{1,0:T(8,128)S(1)}, f32[512,128]{1,0:T(8,128)}, u32[]{:S(2)}) copy-start(f32[512,128]{1,0:T(8,128)} %z_ref.1) | copy-start | bytes 786436
  42.6 15.3 %collective-permute-start.2 = (f32[136,256]{1,0:T(8,128)S(1)}, f32[136,256]{1,0:T(8,128)S(1)}, u32[]{:S(2)}, u32[]{:S(2)}) collective-permute-start(f32[136,256]{1,0:T(8,128)S(1)} %get-tuple-element.28.c_ref), channel_id=1, source_target_pairs={{0,64},{64,0},{1,65},{65,1},{2,66},{66,2},{3,67},{67,3},{4,68},{68... | collective-permute-start | bytes 417800 | tf_op jit(solution)/shard_map/ppermute | solution.py:236
  46.3 11.6 %collective-permute-start.3 = (f32[136,256]{1,0:T(8,128)S(1)}, f32[136,256]{1,0:T(8,128)S(1)}, u32[]{:S(2)}, u32[]{:S(2)}) collective-permute-start(f32[136,256]{1,0:T(8,128)S(1)} %get-tuple-element.29.x_ref), channel_id=1, source_target_pairs={{64,128},{128,64},{65,129},{129,65},{66,130},{130,66},{67,131},{13... | collective-permute-start | bytes 417800 | tf_op jit(solution)/shard_map/ppermute | solution.py:240
  55.0 6.8 %collective-permute-start = (f32[256,128]{1,0:T(8,128)S(1)}, f32[256,128]{1,0:T(8,128)S(1)}, u32[]{:S(2)}, u32[]{:S(2)}) collective-permute-start(f32[256,128]{1,0:T(8,128)S(1)} %get-tuple-element.26.c_ref), channel_id=1, source_target_pairs={{0,64},{64,0},{1,65},{65,1},{2,66},{66,2},{3,67},{67,3},{4,68},{68... | collective-permute-start | bytes 393224 | tf_op jit(solution)/shard_map/ppermute | solution.py:236
  55.1 7.8 %collective-permute-start.1 = (f32[256,128]{1,0:T(8,128)S(1)}, f32[256,128]{1,0:T(8,128)S(1)}, u32[]{:S(2)}, u32[]{:S(2)}) collective-permute-start(f32[256,128]{1,0:T(8,128)S(1)} %get-tuple-element.27.x_ref), channel_id=1, source_target_pairs={{64,128},{128,64},{65,129},{129,65},{66,130},{130,66},{67,131},{13... | collective-permute-start | bytes 393224 | tf_op jit(solution)/shard_map/ppermute | solution.py:240

commit v2 on v1

--- a/solution.py
+++ b/solution.py
@@ -74,12 +74,23 @@
             )
         )
     span = Q
-    rows, cols = iota((H, H), 0), iota((H, H), 1)
     while span < H:
-        corner = ((rows & span) == 0) & ((cols & span) != 0)
-        corner = corner & ((rows & ~(2 * span - 1)) == (cols & ~(2 * span - 1)))
-        parts = [exact(t, jnp.where(corner, v, 0.0)) for t, v in zip(out, blocks)]
-        out = [t - exact(part, t) for t, part in zip(out, parts)]
+        starts = range(0, H, 2 * span)
+
+        def chosen(value):
+            return jnp.concatenate([value[i : i + span] for i in starts], axis=0)
+
+        def placed(value):
+            gap, strips = jnp.zeros((span, H), F32), []
+            for i in range(len(starts)):
+                strips += [value[i * span : (i + 1) * span], gap]
+            return jnp.concatenate(strips, axis=0)
+
+        rows, cols = iota((H // 2, H), 0), iota((H // 2, H), 1)
+        corner = ((cols & span) != 0) & (rows // span == cols // (2 * span))
+        parts = [exact(jnp.where(corner, chosen(v), 0.0), t) for t, v in zip(out, blocks)]
+        parts = [exact(chosen(t), placed(part)) for t, part in zip(out, parts)]
+        out = [t - placed(part) for t, part in zip(out, parts)]
         span *= 2
     return out
 
@@ -154,21 +165,18 @@
         start = stop
 
 
-def gram_kernel(core_ref, g_ref, c_ref, x_ref, yh_ref, yl_ref, th_ref, tl_ref):
+def first_kernel(core_ref, g_ref, z_ref, out_ref, pc_ref, px_ref, c_ref, x_ref, ah_ref, al_ref):
+    first = core_ref[0] == 0
     rows = panel(g_ref, 1)
-    packed = []
+    packed, turned = [], []
     for k, half in enumerate((rows[:R], with_eye(rows[R:]))):
         y, t = halves(half), halves(half.T)
         packed.append(pack(product(t, y)))
-        yh_ref[k], yl_ref[k] = y
-        th_ref[k], tl_ref[k] = t
+        turned.append(t)
+        ah_ref[k], al_ref[k] = y
     up, low = packed
-    first = core_ref[0] == 0
     c_ref[...] = jnp.where(first, low, up)
     x_ref[...] = jnp.where(first, up, low)
-
-
-def first_kernel(core_ref, g_ref, z_ref, th_ref, tl_ref, out_ref, c_ref, x_ref):
     y = with_eye(panel(g_ref, 0))
     yh, yt = halves(y), halves(y.T)
     z = z_ref[...]
@@ -176,21 +184,23 @@
     (t,) = inverses_of([full_parts(product(yt, yh))])
     x = exact(t, p)
     z = z - product(yh, halves(x))
-    up = product((th_ref[0], tl_ref[0]), halves(z[:R]))
-    low = product((th_ref[1], tl_ref[1]), halves(z[R:]))
-    first = core_ref[0] == 0
-    c_ref[...] = jnp.where(first, low, up)
-    x_ref[...] = jnp.where(first, up, low)
     out_ref[...] = z
-
-
-def second_kernel(core_ref, g_ref, c_ref, c_in_ref, x_ref, x_in_ref, th_ref, tl_ref, t_ref, tc_ref, tx_ref):
+    up = product(turned[0], halves(z[:R]))
+    low = product(turned[1], halves(z[R:]))
+    pc_ref[...] = jnp.where(first, low, up)
+    px_ref[...] = jnp.where(first, up, low)
+
+
+def third_kernel(g_ref, th_ref, tl_ref, t_ref):
     y = with_eye(panel(g_ref, 0))
     yh, yt = halves(y), halves(y.T)
     th_ref[...], tl_ref[...] = yt
-    t_ref[...], tc_ref[...], tx_ref[...] = inverses_of(
+    (t_ref[...],) = inverses_of([full_parts(product(yt, yh))])
+
+
+def second_kernel(core_ref, c_ref, c_in_ref, x_ref, x_in_ref, tc_ref, tx_ref):
+    tc_ref[...], tx_ref[...] = inverses_of(
         [
-            full_parts(product(yt, yh)),
             packed_parts(c_ref[...] + c_in_ref[...], True),
             packed_parts(x_ref[...] + x_in_ref[...], core_ref[1] != 0),
         ]
@@ -224,7 +234,6 @@
         out_specs=[VM] * len(outs),
         cost_estimate=pl.CostEstimate(flops=flops, bytes_accessed=1 << 20, transcendentals=0),
         compiler_params=pltpu.CompilerParams(vmem_limit_bytes=12 << 20),
-        name=kernel.__name__,
     )(*args)
 
 
@@ -244,6 +253,7 @@
     core = lax.axis_index("core")
     group = lax.axis_index("xh") * 2 + core
     flags = jnp.stack([core, (group == 1) | (group == 2)]).astype(jnp.int32)
+    panels, flags = lax.optimization_barrier((panels, flags))
     (stack,) = call(spread_kernel, [(8, *panels.shape)], [panels], 10**6)
     near = exchange(stack, "z")
     early, late = call(
@@ -254,25 +264,17 @@
     columns = eigen_rows.shape[1]
     half = ((2, R, R), BF16)
     big = 10**9
-    c, x, ah, al, bh, bl = call(
-        gram_kernel, [(H + 8, R)] * 2 + [half] * 4, [flags, every], big, 1
-    )
-    x_in, c_in = swap_middle(x), swap_cores(c)
-    z, pc, px = call(
+    z, pc, px, c, x, ah, al = call(
         first_kernel,
-        [eigen_rows.shape, (R, columns), (R, columns)],
-        [flags, every, eigen_rows, bh, bl],
+        [eigen_rows.shape, (R, columns), (R, columns)] + [(H + 8, R)] * 2 + [half] * 2,
+        [flags, every, eigen_rows],
         8 * big,
         1,
     )
+    x_in, c_in = swap_middle(x), swap_cores(c)
     px_in, pc_in = swap_middle(px), swap_cores(pc)
-    th, tl, t, tc, tx = call(
-        second_kernel,
-        [((R, 2 * R), BF16)] * 2 + [(R, R)] * 3,
-        [flags, third, c, c_in, x, x_in],
-        8 * big,
-        1,
-    )
+    th, tl, t = call(third_kernel, [((R, 2 * R), BF16)] * 2 + [(R, R)], [third], 4 * big)
+    tc, tx = call(second_kernel, [(R, R)] * 2, [flags, c, c_in, x, x_in], 4 * big, 1)
     (out,) = call(
         last_kernel,
         [eigen_rows.shape],

time: 66.8 us -> 67.7 us (1.013)
  blocking collectives: 17.8 us -> 35.7 us
  waiting for transfers between devices: 14.2 us -> 1.06 us
  starting transfers between devices: 19.4 us -> 15.6 us
    all_to_all x1 -> x2, blocking collectives: 17.8 us -> 35.7 us  [exchange(): return lax.all_to_all(stack, axes, split_axis=0, concat_axis=0, tiled=True)]
    all_to_all x2 -> x1, waiting for transfers between devices: 13.1 us -> 0.01 us  [exchange(): return lax.all_to_all(stack, axes, split_axis=0, concat_axis=0, tiled=True)]
    all_to_all x2 -> x1, starting transfers between devices: 8.61 us -> 3.62 us  [exchange(): return lax.all_to_all(stack, axes, split_axis=0, concat_axis=0, tiled=True)]
    ppermute x2, starting transfers between devices: 7.05 us -> 8.18 us  [swap_middle(): return lax.ppermute(value, ('xh', 'core'), [(1, 2), (2, 1)])]
  transfers between devices with their start and end apart: 6 -> 5, of which waited for: 2 -> 1; matrix products, arithmetic and copies ran while one was open for 0% -> 0% of each run, Pallas kernels for 14% -> 14%
where the time goes in v2:
time: 67.7 us; the launch traced here: 67.4 us
  blocking collectives  35.7 us (53%)
  starting transfers between devices  15.6 us (23%)
  Pallas kernels  14.1 us (21%)
  waiting for transfers between devices  1.06 us (2%)
    all_to_all x2, blocking collectives, exchange(): return lax.all_to_all(stack, axes, split_axis=0, concat_axis=0, tiled=True)  35.7 us
    pallas_call x6, Pallas kernels, call(): pl.pallas_call(kernel, out_shape=[jax.ShapeDtypeStruct(s, d) for s, d in...  14.1 us
    ppermute x2, starting transfers between devices, swap_middle(): return lax.ppermute(value, ('xh', 'core'), [(1, 2), (2, 1)])  8.18 us
    ppermute x2, starting transfers between devices, swap_cores(): return lax.ppermute(value, 'core', [(0, 1), (1, 0)])  3.82 us
    all_to_all x1, starting transfers between devices, exchange(): return lax.all_to_all(stack, axes, split_axis=0, concat_axis=0, tiled=True)  3.62 us
  transfers between devices with their start and end apart: 5, of which 1 were waited for; matrix products, arithmetic and copies ran while one was open for 0% of the time, Pallas kernels for 14%

profile of v2, /device:TPU:1, one launch (start us, length us, event | category | flops | bytes accessed | tf_op | source)
XLA Modules:
  0.0 67.4 jit_solution(15538896883994398880)
XLA Ops:
  0.0 0.0 copy-start
  0.0 0.1 pad_add_fusion.core_ref
  0.1 0.7 copy-done
  0.8 17.8 %all_to_all.15.value_ref = f32[8,3,8,256]{3,2,1,0:T(8,128)S(1)} all-to-all(f32[8,3,8,256]{3,2,1,0:T(8,128)S(1)} %shard_map.28), channel_id=1, replica_groups=mesh['xh'=2,'core'=2,'y'=4,'xl'=2,'z'=8] {'z'}, dimensions={0} | all-to-all | bytes 393216 | tf_op jit(solution)/shard_map/all_to_all | solution.py:241
  18.5 0.9 %shard_map.29 = (f32[8,8,2,8,256]{4,3,2,1,0:T(8,128)S(1)}, f32[8,8,1,8,256]{4,3,2,1,0:T(8,128)}) custom-call(f32[8,3,8,256]{3,2,1,0:T(8,128)S(1)} %all_to_all.15.value_ref), custom_call_target="tpu_custom_call" | custom-call | flops 1000000 | bytes 1048576 | tf_op jit(solution)/shard_map/pallas_call | solution.py:230
  19.4 17.9 %all_to_all.16.g_ref = f32[8,8,2,8,256]{4,3,2,1,0:T(8,128)S(1)} all-to-all(f32[8,8,2,8,256]{4,3,2,1,0:T(8,128)S(1)} %get-tuple-element.24), channel_id=1, replica_groups=mesh['xh'=2,'core'=2,'y'=4,'xl'=2,'z'=8] {'y','xl'}, dimensions={0} | all-to-all | bytes 2097152 | tf_op jit(solution)/shard_map/all_to_all | solution.py:241
  37.4 0.0 copy-start.1
  37.4 3.6 %all-to-all-start.1 = ((f32[8,8,1,8,256]{4,3,2,1,0:T(8,128)}), f32[8,8,1,8,256]{4,3,2,1,0:T(8,128)S(1)}, u32[]{:S(2)}, u32[]{:S(2)}) async-start(f32[8,8,1,8,256]{4,3,2,1,0:T(8,128)} %get-tuple-element.23), calls=%async_computation.1 | async-start | bytes 1048576 | tf_op jit(solution)/shard_map/all_to_all | solution.py:241
  41.0 0.0 copy-done.1
  41.0 4.6 %shard_map.30 = (f32[512,128]{1,0:T(8,128)S(1)}, f32[256,128]{1,0:T(8,128)S(1)}, f32[256,128]{1,0:T(8,128)S(1)}, f32[136,256]{1,0:T(8,128)S(1)}, f32[136,256]{1,...) custom-call(s32[2]{0:T(128)S(1)} %pad_add_fusion.core_ref, ...), custom_call_target="tpu_custom_call" | custom-call | flops 8000000000 | bytes 1048576 | tf_op jit(solution)/shard_map/pallas_call | solution.py:230
  45.6 3.7 %collective-permute-start.2 = (f32[136,256]{1,0:T(8,128)S(1)}, f32[136,256]{1,0:T(8,128)S(1)}, u32[]{:S(2)}, u32[]{:S(2)}) collective-permute-start(f32[136,256]{1,0:T(8,128)S(1)} %get-tuple-element.28.c_ref), channel_id=1, source_target_pairs={{0,64},{64,0},{1,65},{65,1},{2,66},{66,2},{3,67},{67,3},{4,68},{68... | collective-permute-start | bytes 417800 | tf_op jit(solution)/shard_map/ppermute | solution.py:245
  49.3 4.3 %collective-permute-start.3 = (f32[136,256]{1,0:T(8,128)S(1)}, f32[136,256]{1,0:T(8,128)S(1)}, u32[]{:S(2)}, u32[]{:S(2)}) collective-permute-start(f32[136,256]{1,0:T(8,128)S(1)} %get-tuple-element.29.x_ref), channel_id=1, source_target_pairs={{64,128},{128,64},{65,129},{129,65},{66,130},{130,66},{67,131},{13... | collective-permute-start | bytes 417800 | tf_op jit(solution)/shard_map/ppermute | solution.py:249
  53.6 0.0 all-to-all-done.1.g_ref
  53.6 2.3 %shard_map.32 = (bf16[256,512]{1,0:T(8,128)(2,1)S(1)}, bf16[256,512]{1,0:T(8,128)(2,1)S(1)}, f32[256,256]{1,0:T(8,128)S(1)}) custom-call(f32[8,8,1,8,256]{4,3,2,1,0:T(8,128)S(1)} %all-to-all-done.1.g_ref), custom_call_target="tpu_custom_call" | custom-call | flops 4000000000 | bytes 1048576 | tf_op jit(solution)/shard_map/pallas_call | solution.py:230
  55.9 0.1 collective-permute-start
  56.0 3.9 %collective-permute-start.1 = (f32[256,128]{1,0:T(8,128)S(1)}, f32[256,128]{1,0:T(8,128)S(1)}, u32[]{:S(2)}, u32[]{:S(2)}) collective-permute-start(f32[256,128]{1,0:T(8,128)S(1)} %get-tuple-element.27.x_ref), channel_id=1, source_target_pairs={{64,128},{128,64},{65,129},{129,65},{66,130},{130,66},{67,131},{13... | collective-permute-start | bytes 393224 | tf_op jit(solution)/shard_map/ppermute | solution.py:249
  59.9 0.0 collective-permute-done.2.c_in_ref
  60.0 0.0 collective-permute-done.3.x_in_ref
  60.0 2.8 %shard_map.31 = (f32[256,256]{1,0:T(8,128)S(1)}, f32[256,256]{1,0:T(8,128)S(1)}) custom-call(s32[2]{0:T(128)S(1)} %pad_add_fusion.core_ref, f32[136,256]{1,0:T(8,128)S(1)} %get-tuple-element.28.c_ref, f32[136,256]{1,0:T(8,128)S(1)} %collective-permute-done.2.c_in_ref, f32[136,256]{1,0:T(8,128)S(1)} %get-tuple-element.29.x_ref, ...), custom_call_target="tpu_custom_call" | custom-call | flops 4000000000 | bytes 1048576 | tf_op jit(solution)/shard_map/pallas_call | solution.py:230
  62.7 0.0 collective-permute-done.c_in_ref
  62.7 1.1 %collective-permute-done.1.x_in_ref = f32[256,128]{1,0:T(8,128)S(1)} collective-permute-done((f32[256,128]{1,0:T(8,128)S(1)}, f32[256,128]{1,0:T(8,128)S(1)}, u32[]{:S(2)}, u32[]{:S(2)}) %collective-permute-start.1) | collective-permute-done | bytes 131104 | tf_op jit(solution)/shard_map/ppermute | solution.py:249
  63.8 3.6 %shard_map.33 = f32[512,128]{1,0:T(8,128)} custom-call(s32[2]{0:T(128)S(1)} %pad_add_fusion.core_ref, f32[8,8,1,8,256]{4,3,2,1,0:T(8,128)S(1)} %all-to-all-done.1.g_ref, f32[512,128]{1,0:T(8,128)S(1)} %get-tuple-element.25.z_ref, f32[256,128]{1,0:T(8,128)S(1)} %get-tuple-element.26.c_ref, f32[256,128]{1,0:T(8,128)S(1)} %collective-permute-done.c_in_ref, ...), custom_call_target="tpu_custom_call" | custom-call | flops 2000000000 | bytes 1048576 | tf_op jit(solution)/shard_map/pallas_call | solution.py:230
  (1 shorter events, 0.0 us)
Async XLA Ops:
  0.0 0.7 %copy-start = (f32[3,8,256]{2,1,0:T(8,128)S(1)}, f32[3,8,256]{2,1,0:T(8,128)}, u32[]{:S(2)}) copy-start(f32[3,8,256]{2,1,0:T(8,128)} %value_ref) | copy-start | bytes 73732
  37.4 3.6 %copy-start.1 = (f32[512,128]{1,0:T(8,128)S(1)}, f32[512,128]{1,0:T(8,128)}, u32[]{:S(2)}) copy-start(f32[512,128]{1,0:T(8,128)} %z_ref.1) | copy-start | bytes 786436
  37.4 16.2 %all-to-all-start.1 = ((f32[8,8,1,8,256]{4,3,2,1,0:T(8,128)}), f32[8,8,1,8,256]{4,3,2,1,0:T(8,128)S(1)}, u32[]{:S(2)}, u32[]{:S(2)}) async-start(f32[8,8,1,8,256]{4,3,2,1,0:T(8,128)} %get-tuple-element.23), calls=%async_computation.1 | async-start | bytes 1048576 | tf_op jit(solution)/shard_map/all_to_all | solution.py:241
  45.6 14.4 %collective-permute-start.2 = (f32[136,256]{1,0:T(8,128)S(1)}, f32[136,256]{1,0:T(8,128)S(1)}, u32[]{:S(2)}, u32[]{:S(2)}) collective-permute-start(f32[136,256]{1,0:T(8,128)S(1)} %get-tuple-element.28.c_ref), channel_id=1, source_target_pairs={{0,64},{64,0},{1,65},{65,1},{2,66},{66,2},{3,67},{67,3},{4,68},{68... | collective-permute-start | bytes 417800 | tf_op jit(solution)/shard_map/ppermute | solution.py:245
  49.3 10.7 %collective-permute-start.3 = (f32[136,256]{1,0:T(8,128)S(1)}, f32[136,256]{1,0:T(8,128)S(1)}, u32[]{:S(2)}, u32[]{:S(2)}) collective-permute-start(f32[136,256]{1,0:T(8,128)S(1)} %get-tuple-element.29.x_ref), channel_id=1, source_target_pairs={{64,128},{128,64},{65,129},{129,65},{66,130},{130,66},{67,131},{13... | collective-permute-start | bytes 417800 | tf_op jit(solution)/shard_map/ppermute | solution.py:249
  55.9 6.8 %collective-permute-start = (f32[256,128]{1,0:T(8,128)S(1)}, f32[256,128]{1,0:T(8,128)S(1)}, u32[]{:S(2)}, u32[]{:S(2)}) collective-permute-start(f32[256,128]{1,0:T(8,128)S(1)} %get-tuple-element.26.c_ref), channel_id=1, source_target_pairs={{0,64},{64,0},{1,65},{65,1},{2,66},{66,2},{3,67},{67,3},{4,68},{68... | collective-permute-start | bytes 393224 | tf_op jit(solution)/shard_map/ppermute | solution.py:245
  56.0 7.8 %collective-permute-start.1 = (f32[256,128]{1,0:T(8,128)S(1)}, f32[256,128]{1,0:T(8,128)S(1)}, u32[]{:S(2)}, u32[]{:S(2)}) collective-permute-start(f32[256,128]{1,0:T(8,128)S(1)} %get-tuple-element.27.x_ref), channel_id=1, source_target_pairs={{64,128},{128,64},{65,129},{129,65},{66,130},{130,66},{67,131},{13... | collective-permute-start | bytes 393224 | tf_op jit(solution)/shard_map/ppermute | solution.py:249

commit v3 on v2

--- a/solution.py
+++ b/solution.py
@@ -22,11 +22,31 @@
 
 
 def product(a, b):
-    return dot(a[0], b[0]) + (dot(a[0], b[1]) + dot(a[1], b[0]))
+    if b[0].shape[1] > H:
+        return dot(a[0], b[0]) + (dot(a[0], b[1]) + dot(a[1], b[0]))
+    both = dot(a[0], jnp.concatenate(b, axis=1))
+    return both[:, :H] + (both[:, H:] + dot(a[1], b[0]))
+
+
+def thirds(value):
+    top = value.astype(BF16)
+    rest = value - top.astype(F32)
+    middle = rest.astype(BF16)
+    return top, middle, (rest - middle.astype(F32)).astype(BF16)
 
 
 def exact(a, b):
-    return jnp.dot(a, b, precision=lax.Precision.HIGHEST, preferred_element_type=F32)
+    a0, a1, a2 = thirds(a)
+    b0, b1, b2 = thirds(b)
+    small = dot(jnp.concatenate([a0, a2], axis=1), jnp.concatenate([b2, b0], axis=0))
+    pair = jnp.concatenate([b0, b1], axis=1)
+    if a.shape[1] > H:
+        first, second = dot(a0, pair), dot(a1, pair)
+        cross = first[:, H:] + second[:, :H]
+        return first[:, :H] + (cross + (second[:, H:] + small))
+    swapped = jnp.concatenate([b1, b0], axis=1)
+    both = dot(jnp.concatenate([a0, a1], axis=1), jnp.concatenate([pair, swapped], axis=0))
+    return both[:, :H] + (both[:, H:] + small)
 
 
 def iota(shape, dim):
@@ -103,18 +123,26 @@
     return list(zip(tops, corners, bottoms))
 
 
-def inverses_of(grams):
+def scaled(parts):
+    g00, g01, g11, d00, d11 = parts
     above = iota((H, H), 0) < iota((H, H), 1)
     eye = iota((H, H), 0) == iota((H, H), 1)
-    units, scales = [], []
-    for g00, g01, g11, d00, d11 in grams:
-        r0, r1 = 2.0 / d00, 2.0 / d11
-        units.append(
-            (jnp.where(above, g00 * r0, 0.0), g01 * r1, jnp.where(above, g11 * r1, 0.0))
-        )
-        scales.append(
-            [jnp.sum(jnp.where(eye, r, 0.0), axis=1, keepdims=True) for r in (r0, r1)]
-        )
+    r0, r1 = 2.0 / d00, 2.0 / d11
+    unit = jnp.where(above, g00 * r0, 0.0), g01 * r1, jnp.where(above, g11 * r1, 0.0)
+    scale = [jnp.sum(jnp.where(eye, r, 0.0), axis=1, keepdims=True) for r in (r0, r1)]
+    return unit, scale
+
+
+def solve(parts, p):
+    (v00, v01, v11), (c0, c1) = scaled(parts)
+    t00, t11 = invert_units([v00, v11])
+    x1 = exact(t11, p[H:])
+    x0 = exact(t00, p[:H] - exact(v01, x1))
+    return jnp.concatenate([x0 * c0, x1 * c1], axis=0)
+
+
+def inverses_of(grams):
+    units, scales = zip(*[scaled(parts) for parts in grams])
     out = []
     for (t00, t01, t11), (c0, c1) in zip(invert_unit_all(units), scales):
         top = jnp.concatenate([t00 * c0, t01 * c0], axis=1)
@@ -165,8 +193,23 @@
         start = stop
 
 
-def first_kernel(core_ref, g_ref, z_ref, out_ref, pc_ref, px_ref, c_ref, x_ref, ah_ref, al_ref):
-    first = core_ref[0] == 0
+def in_middle():
+    return lax.axis_index("xh") != lax.axis_index("core")
+
+
+def store_by_core(core, low, up, c_ref, x_ref):
+    @pl.when(core == 0)
+    def _():
+        c_ref[...] = low
+        x_ref[...] = up
+
+    @pl.when(core != 0)
+    def _():
+        c_ref[...] = up
+        x_ref[...] = low
+
+
+def first_kernel(g_ref, z_ref, out_ref, pc_ref, px_ref, c_ref, x_ref, ah_ref, al_ref):
     rows = panel(g_ref, 1)
     packed, turned = [], []
     for k, half in enumerate((rows[:R], with_eye(rows[R:]))):
@@ -174,48 +217,41 @@
         packed.append(pack(product(t, y)))
         turned.append(t)
         ah_ref[k], al_ref[k] = y
-    up, low = packed
-    c_ref[...] = jnp.where(first, low, up)
-    x_ref[...] = jnp.where(first, up, low)
     y = with_eye(panel(g_ref, 0))
     yh, yt = halves(y), halves(y.T)
     z = z_ref[...]
     p = product(yt, halves(z))
-    (t,) = inverses_of([full_parts(product(yt, yh))])
-    x = exact(t, p)
+    x = solve(full_parts(product(yt, yh)), p)
     z = z - product(yh, halves(x))
     out_ref[...] = z
     up = product(turned[0], halves(z[:R]))
     low = product(turned[1], halves(z[R:]))
-    pc_ref[...] = jnp.where(first, low, up)
-    px_ref[...] = jnp.where(first, up, low)
-
-
-def third_kernel(g_ref, th_ref, tl_ref, t_ref):
+    store_by_core(lax.axis_index("core"), low, up, pc_ref, px_ref)
+    store_by_core(lax.axis_index("core"), packed[1], packed[0], c_ref, x_ref)
+
+
+def second_kernel(g_ref, c_ref, c_in_ref, x_ref, x_in_ref, th_ref, tl_ref, t_ref, tc_ref, tx_ref):
     y = with_eye(panel(g_ref, 0))
     yh, yt = halves(y), halves(y.T)
     th_ref[...], tl_ref[...] = yt
-    (t_ref[...],) = inverses_of([full_parts(product(yt, yh))])
-
-
-def second_kernel(core_ref, c_ref, c_in_ref, x_ref, x_in_ref, tc_ref, tx_ref):
-    tc_ref[...], tx_ref[...] = inverses_of(
+    t_ref[...], tc_ref[...], tx_ref[...] = inverses_of(
         [
+            full_parts(product(yt, yh)),
             packed_parts(c_ref[...] + c_in_ref[...], True),
-            packed_parts(x_ref[...] + x_in_ref[...], core_ref[1] != 0),
+            packed_parts(x_ref[...] + x_in_ref[...], in_middle()),
         ]
     )
 
 
-def last_kernel(core_ref, g_ref, z_ref, c_ref, c_in_ref, x_ref, x_in_ref, tc_ref, tx_ref,
+def last_kernel(g_ref, z_ref, c_ref, c_in_ref, x_ref, x_in_ref, tc_ref, tx_ref,
                 ah_ref, al_ref, th_ref, tl_ref, t_ref, out_ref):
     xc = exact(tc_ref[...], c_ref[...] + c_in_ref[...])
     xx = exact(tx_ref[...], x_ref[...] + x_in_ref[...])
-    xx = jnp.where(core_ref[1] != 0, xx, 0.0)
-    first = core_ref[0] == 0
-    z_up = z_ref[:R] - product((ah_ref[0], al_ref[0]), halves(jnp.where(first, xx, xc)))
-    z_low = z_ref[R:] - product((ah_ref[1], al_ref[1]), halves(jnp.where(first, xc, xx)))
-    z = jnp.concatenate([z_up, z_low], axis=0)
+    xx = jnp.where(in_middle(), xx, 0.0)
+    for half, x in ((1 - lax.axis_index("core"), xc), (lax.axis_index("core"), xx)):
+        rows = pl.ds(pl.multiple_of(half * R, R), R)
+        out_ref[rows, :] = z_ref[rows, :] - product((ah_ref[half], al_ref[half]), halves(x))
+    z = out_ref[...]
     p = product((th_ref[...], tl_ref[...]), halves(z))
     x = exact(t_ref[...], p)
     out_ref[...] = z - product(halves(with_eye(panel(g_ref, 0))), halves(x))
@@ -250,10 +286,6 @@
 
 
 def local(eigen_rows, panels):
-    core = lax.axis_index("core")
-    group = lax.axis_index("xh") * 2 + core
-    flags = jnp.stack([core, (group == 1) | (group == 2)]).astype(jnp.int32)
-    panels, flags = lax.optimization_barrier((panels, flags))
     (stack,) = call(spread_kernel, [(8, *panels.shape)], [panels], 10**6)
     near = exchange(stack, "z")
     early, late = call(
@@ -267,20 +299,22 @@
     z, pc, px, c, x, ah, al = call(
         first_kernel,
         [eigen_rows.shape, (R, columns), (R, columns)] + [(H + 8, R)] * 2 + [half] * 2,
-        [flags, every, eigen_rows],
+        [every, eigen_rows],
         8 * big,
-        1,
     )
     x_in, c_in = swap_middle(x), swap_cores(c)
     px_in, pc_in = swap_middle(px), swap_cores(pc)
-    th, tl, t = call(third_kernel, [((R, 2 * R), BF16)] * 2 + [(R, R)], [third], 4 * big)
-    tc, tx = call(second_kernel, [(R, R)] * 2, [flags, c, c_in, x, x_in], 4 * big, 1)
+    th, tl, t, tc, tx = call(
+        second_kernel,
+        [((R, 2 * R), BF16)] * 2 + [(R, R)] * 3,
+        [third, c, c_in, x, x_in],
+        8 * big,
+    )
     (out,) = call(
         last_kernel,
         [eigen_rows.shape],
-        [flags, third, z, pc, pc_in, px, px_in, tc, tx, ah, al, th, tl, t],
+        [third, z, pc, pc_in, px, px_in, tc, tx, ah, al, th, tl, t],
         2 * big,
-        1,
     )
     return out
 

time: 67.7 us -> 62.7 us (0.926)
  Pallas kernels: 14.1 us -> 9.28 us
  starting transfers between devices: 15.6 us -> 14.5 us
  waiting for transfers between devices: 1.06 us -> 2.04 us
    pallas_call x6 -> x5, Pallas kernels: 14.1 us -> 9.28 us  [call(): pl.pallas_call(kernel, out_shape=[jax.ShapeDtypeStruct(s, d) for s, d in...]
    ppermute x2, starting transfers between devices: 8.18 us -> 7.05 us  [swap_middle(): return lax.ppermute(value, ('xh', 'core'), [(1, 2), (2, 1)])]
    ppermute x2, waiting for transfers between devices: 1.05 us -> 2.03 us  [swap_middle(): return lax.ppermute(value, ('xh', 'core'), [(1, 2), (2, 1)])]
  transfers between devices with their start and end apart: 5 -> 5, of which waited for: 1 -> 2; matrix products, arithmetic and copies ran while one was open for 0% -> 0% of each run, Pallas kernels for 14% -> 10%
where the time goes in v3:
time: 62.7 us; the launch traced here: 62.3 us
  blocking collectives  35.7 us (57%)
  starting transfers between devices  14.5 us (23%)
  Pallas kernels  9.28 us (15%)
  waiting for transfers between devices  2.04 us (3%)
  local copies, waits for them, and re-layouts  0.74 us (1%)
    all_to_all x2, blocking collectives, exchange(): return lax.all_to_all(stack, axes, split_axis=0, concat_axis=0, tiled=True)  35.7 us
    pallas_call x5, Pallas kernels, call(): pl.pallas_call(kernel, out_shape=[jax.ShapeDtypeStruct(s, d) for s, d in...  9.28 us
    ppermute x2, starting transfers between devices, swap_middle(): return lax.ppermute(value, ('xh', 'core'), [(1, 2), (2, 1)])  7.05 us
    ppermute x2, starting transfers between devices, swap_cores(): return lax.ppermute(value, 'core', [(0, 1), (1, 0)])  3.82 us
    all_to_all x1, starting transfers between devices, exchange(): return lax.all_to_all(stack, axes, split_axis=0, concat_axis=0, tiled=True)  3.62 us
    ppermute x2, waiting for transfers between devices, swap_middle(): return lax.ppermute(value, ('xh', 'core'), [(1, 2), (2, 1)])  2.03 us
  transfers between devices with their start and end apart: 5, of which 2 were waited for; matrix products, arithmetic and copies ran while one was open for 0% of the time, Pallas kernels for 10%

profile of v3, /device:TPU:1, one launch (start us, length us, event | category | flops | bytes accessed | tf_op | source)
XLA Modules:
  0.0 62.3 jit_solution(17224688441930329571)
XLA Ops:
  0.0 0.0 copy-start
  0.0 0.7 %copy-done = f32[3,8,256]{2,1,0:T(8,128)S(1)} copy-done((f32[3,8,256]{2,1,0:T(8,128)S(1)}, f32[3,8,256]{2,1,0:T(8,128)}, u32[]{:S(2)}) %copy-start) | copy-done | bytes 24600
  0.8 17.8 %all_to_all.15.value_ref = f32[8,3,8,256]{3,2,1,0:T(8,128)S(1)} all-to-all(f32[8,3,8,256]{3,2,1,0:T(8,128)S(1)} %shard_map.28), channel_id=1, replica_groups=mesh['xh'=2,'core'=2,'y'=4,'xl'=2,'z'=8] {'z'}, dimensions={0} | all-to-all | bytes 393216 | tf_op jit(solution)/shard_map/all_to_all | solution.py:277
  18.5 0.9 %shard_map.29 = (f32[8,8,2,8,256]{4,3,2,1,0:T(8,128)S(1)}, f32[8,8,1,8,256]{4,3,2,1,0:T(8,128)}) custom-call(f32[8,3,8,256]{3,2,1,0:T(8,128)S(1)} %all_to_all.15.value_ref), custom_call_target="tpu_custom_call" | custom-call | flops 1000000 | bytes 1048576 | tf_op jit(solution)/shard_map/pallas_call | solution.py:266
  19.4 17.9 %all_to_all.16.g_ref = f32[8,8,2,8,256]{4,3,2,1,0:T(8,128)S(1)} all-to-all(f32[8,8,2,8,256]{4,3,2,1,0:T(8,128)S(1)} %get-tuple-element.20), channel_id=1, replica_groups=mesh['xh'=2,'core'=2,'y'=4,'xl'=2,'z'=8] {'y','xl'}, dimensions={0} | all-to-all | bytes 2097152 | tf_op jit(solution)/shard_map/all_to_all | solution.py:277
  37.4 0.0 copy-start.1
  37.4 3.6 %all-to-all-start.1 = ((f32[8,8,1,8,256]{4,3,2,1,0:T(8,128)}), f32[8,8,1,8,256]{4,3,2,1,0:T(8,128)S(1)}, u32[]{:S(2)}, u32[]{:S(2)}) async-start(f32[8,8,1,8,256]{4,3,2,1,0:T(8,128)} %get-tuple-element.19), calls=%async_computation.1 | async-start | bytes 1048576 | tf_op jit(solution)/shard_map/all_to_all | solution.py:277
  41.0 0.0 copy-done.1
  41.0 3.2 %shard_map.30 = (f32[512,128]{1,0:T(8,128)S(1)}, f32[256,128]{1,0:T(8,128)S(1)}, f32[256,128]{1,0:T(8,128)S(1)}, f32[136,256]{1,0:T(8,128)S(1)}, f32[136,256]{1,...) custom-call(f32[8,8,2,8,256]{4,3,2,1,0:T(8,128)S(1)} %all_to_all.16.g_ref, ...), custom_call_target="tpu_custom_call" | custom-call | flops 8000000000 | bytes 1048576 | tf_op jit(solution)/shard_map/pallas_call | solution.py:266
  44.2 3.7 %collective-permute-start.2 = (f32[136,256]{1,0:T(8,128)S(1)}, f32[136,256]{1,0:T(8,128)S(1)}, u32[]{:S(2)}, u32[]{:S(2)}) collective-permute-start(f32[136,256]{1,0:T(8,128)S(1)} %get-tuple-element.24.c_ref), channel_id=1, source_target_pairs={{0,64},{64,0},{1,65},{65,1},{2,66},{66,2},{3,67},{67,3},{4,68},{68... | collective-permute-start | bytes 417800 | tf_op jit(solution)/shard_map/ppermute | solution.py:281
  48.0 4.3 %collective-permute-start.3 = (f32[136,256]{1,0:T(8,128)S(1)}, f32[136,256]{1,0:T(8,128)S(1)}, u32[]{:S(2)}, u32[]{:S(2)}) collective-permute-start(f32[136,256]{1,0:T(8,128)S(1)} %get-tuple-element.25.x_ref), channel_id=1, source_target_pairs={{64,128},{128,64},{65,129},{129,65},{66,130},{130,66},{67,131},{13... | collective-permute-start | bytes 417800 | tf_op jit(solution)/shard_map/ppermute | solution.py:285
  52.2 0.1 collective-permute-start
  52.3 2.8 %collective-permute-start.1 = (f32[256,128]{1,0:T(8,128)S(1)}, f32[256,128]{1,0:T(8,128)S(1)}, u32[]{:S(2)}, u32[]{:S(2)}) collective-permute-start(f32[256,128]{1,0:T(8,128)S(1)} %get-tuple-element.23.x_ref), channel_id=1, source_target_pairs={{64,128},{128,64},{65,129},{129,65},{66,130},{130,66},{67,131},{13... | collective-permute-start | bytes 393224 | tf_op jit(solution)/shard_map/ppermute | solution.py:285
  55.1 0.0 all-to-all-done.1.g_ref
  55.2 0.0 collective-permute-done.2.c_in_ref
  55.2 0.7 %collective-permute-done.3.x_in_ref = f32[136,256]{1,0:T(8,128)S(1)} collective-permute-done((f32[136,256]{1,0:T(8,128)S(1)}, f32[136,256]{1,0:T(8,128)S(1)}, u32[]{:S(2)}, u32[]{:S(2)}) %collective-permute-start.3) | collective-permute-done | bytes 139296 | tf_op jit(solution)/shard_map/ppermute | solution.py:285
  55.8 2.9 %shard_map.31 = (bf16[256,512]{1,0:T(8,128)(2,1)S(1)}, bf16[256,512]{1,0:T(8,128)(2,1)S(1)}, f32[256,256]{1,0:T(8,128)S(1)}, f32[256,256]{1,0:T(8,128)S(1)}, f32[256,256]{1,0:T(8,128)S(1)}) custom-call(f32[8,8,1,8,256]{4,3,2,1,0:T(8,128)S(1)} %all-to-all-done.1.g_ref, f32[136,256]{1,0:T(8,128)S(1)} %get-tuple-element.24.c_ref, ...), custom_call_target="tpu_custom_call" | custom-call | flops 8000000000 | bytes 1048576 | tf_op jit(solution)/shard_map/pallas_call | solution.py:266
  58.8 0.0 collective-permute-done.c_in_ref
  58.8 1.4 %collective-permute-done.1.x_in_ref = f32[256,128]{1,0:T(8,128)S(1)} collective-permute-done((f32[256,128]{1,0:T(8,128)S(1)}, f32[256,128]{1,0:T(8,128)S(1)}, u32[]{:S(2)}, u32[]{:S(2)}) %collective-permute-start.1) | collective-permute-done | bytes 131104 | tf_op jit(solution)/shard_map/ppermute | solution.py:285
  60.1 2.2 %shard_map.32 = f32[512,128]{1,0:T(8,128)} custom-call(f32[8,8,1,8,256]{4,3,2,1,0:T(8,128)S(1)} %all-to-all-done.1.g_ref, f32[512,128]{1,0:T(8,128)S(1)} %get-tuple-element.21.z_ref, f32[256,128]{1,0:T(8,128)S(1)} %get-tuple-element.22.c_ref, f32[256,128]{1,0:T(8,128)S(1)} %collective-permute-done.c_in_ref, f32[256,128]{1,0:T(8,128)S(1)} %get-tuple-element.23.x_ref, ...), custom_call_target="tpu_custom_call" | custom-call | flops 2000000000 | bytes 1048576 | tf_op jit(solution)/shard_map/pallas_call | solution.py:266
  (1 shorter events, 0.0 us)
Async XLA Ops:
  0.0 0.7 %copy-start = (f32[3,8,256]{2,1,0:T(8,128)S(1)}, f32[3,8,256]{2,1,0:T(8,128)}, u32[]{:S(2)}) copy-start(f32[3,8,256]{2,1,0:T(8,128)} %value_ref.1) | copy-start | bytes 73732
  37.4 3.6 %copy-start.1 = (f32[512,128]{1,0:T(8,128)S(1)}, f32[512,128]{1,0:T(8,128)}, u32[]{:S(2)}) copy-start(f32[512,128]{1,0:T(8,128)} %z_ref.1) | copy-start | bytes 786436
  37.4 17.8 %all-to-all-start.1 = ((f32[8,8,1,8,256]{4,3,2,1,0:T(8,128)}), f32[8,8,1,8,256]{4,3,2,1,0:T(8,128)S(1)}, u32[]{:S(2)}, u32[]{:S(2)}) async-start(f32[8,8,1,8,256]{4,3,2,1,0:T(8,128)} %get-tuple-element.19), calls=%async_computation.1 | async-start | bytes 1048576 | tf_op jit(solution)/shard_map/all_to_all | solution.py:277
  44.2 10.9 %collective-permute-start.2 = (f32[136,256]{1,0:T(8,128)S(1)}, f32[136,256]{1,0:T(8,128)S(1)}, u32[]{:S(2)}, u32[]{:S(2)}) collective-permute-start(f32[136,256]{1,0:T(8,128)S(1)} %get-tuple-element.24.c_ref), channel_id=1, source_target_pairs={{0,64},{64,0},{1,65},{65,1},{2,66},{66,2},{3,67},{67,3},{4,68},{68... | collective-permute-start | bytes 417800 | tf_op jit(solution)/shard_map/ppermute | solution.py:281
  48.0 7.9 %collective-permute-start.3 = (f32[136,256]{1,0:T(8,128)S(1)}, f32[136,256]{1,0:T(8,128)S(1)}, u32[]{:S(2)}, u32[]{:S(2)}) collective-permute-start(f32[136,256]{1,0:T(8,128)S(1)} %get-tuple-element.25.x_ref), channel_id=1, source_target_pairs={{64,128},{128,64},{65,129},{129,65},{66,130},{130,66},{67,131},{13... | collective-permute-start | bytes 417800 | tf_op jit(solution)/shard_map/ppermute | solution.py:285
  52.2 6.5 %collective-permute-start = (f32[256,128]{1,0:T(8,128)S(1)}, f32[256,128]{1,0:T(8,128)S(1)}, u32[]{:S(2)}, u32[]{:S(2)}) collective-permute-start(f32[256,128]{1,0:T(8,128)S(1)} %get-tuple-element.22.c_ref), channel_id=1, source_target_pairs={{0,64},{64,0},{1,65},{65,1},{2,66},{66,2},{3,67},{67,3},{4,68},{68... | collective-permute-start | bytes 393224 | tf_op jit(solution)/shard_map/ppermute | solution.py:281
  52.3 7.8 %collective-permute-start.1 = (f32[256,128]{1,0:T(8,128)S(1)}, f32[256,128]{1,0:T(8,128)S(1)}, u32[]{:S(2)}, u32[]{:S(2)}) collective-permute-start(f32[256,128]{1,0:T(8,128)S(1)} %get-tuple-element.23.x_ref), channel_id=1, source_target_pairs={{64,128},{128,64},{65,129},{129,65},{66,130},{130,66},{67,131},{13... | collective-permute-start | bytes 393224 | tf_op jit(solution)/shard_map/ppermute | solution.py:285
